TPU v7x, 32 devices: a whole 2x2x4 slice. The times are simulated.
32 devices in a mesh: dp: 16 (over z, y, core), fsdp: 2 (over x).
Axes of the slice: x: 2, y: 2, z: 4, core: 2. Of those that a mesh axis runs over, the one named last changes fastest.
Arguments:
- patches: bfloat16 [16384, 768], P(('dp', 'fsdp')), may hold values from -6 to 6
- cotangent: bfloat16 [16384, 768], P(('dp', 'fsdp')), may hold values from -6 to 6
- lengths: int32 [32, 4], P(('dp', 'fsdp')), may hold values from 0 to 512, as said below
- arrange: int32 [16384], P(('dp', 'fsdp')), may hold values from 0 to 511, as said below
- first_gain: bfloat16 [768], P('dp'), may hold values from 0.3984375 to 1.59375
- first_shift: bfloat16 [768], P('dp'), may hold values from -1.5 to 1.5
- project_weight: bfloat16 [768, 2304], P('dp', 'fsdp'), may hold values from -0.21875 to 0.21875
- query_bias: bfloat16 [768], P('dp'), may hold values from -1.5 to 1.5
- value_bias: bfloat16 [768], P('dp'), may hold values from -1.5 to 1.5
- output_weight: bfloat16 [768, 768], P('dp', 'fsdp'), may hold values from -1.75 to 1.75
- output_bias: bfloat16 [768], P('dp'), may hold values from -1.5 to 1.5
- second_gain: bfloat16 [768], P('dp'), may hold values from 0.3984375 to 1.59375
- second_shift: bfloat16 [768], P('dp'), may hold values from -1.5 to 1.5
- up_weight: bfloat16 [768, 3072], P('dp', 'fsdp'), may hold values from -0.21875 to 0.21875
- up_bias: bfloat16 [3072], P('dp'), may hold values from -1.5 to 1.5
- down_weight: bfloat16 [3072, 768], P('dp', 'fsdp'), may hold values from -0.109375 to 0.109375
- down_bias: bfloat16 [768], P('dp'), may hold values from -1.5 to 1.5
Outputs:
- encoded: bfloat16 [16384, 768], P(('dp', 'fsdp'))
- grad_patches: bfloat16 [16384, 768], P(('dp', 'fsdp'))
- grad_first_gain: float32 [768], P('dp')
- grad_first_shift: float32 [768], P('dp')
- grad_project_weight: float32 [768, 2304], P('dp', 'fsdp')
- grad_query_bias: float32 [768], P('dp')
- grad_value_bias: float32 [768], P('dp')
- grad_output_weight: float32 [768, 768], P('dp', 'fsdp')
- grad_output_bias: float32 [768], P('dp')
- grad_second_gain: float32 [768], P('dp')
- grad_second_shift: float32 [768], P('dp')
- grad_up_weight: float32 [768, 3072], P('dp', 'fsdp')
- grad_up_bias: float32 [3072], P('dp')
- grad_down_weight: float32 [3072, 768], P('dp', 'fsdp')
- grad_down_bias: float32 [768], P('dp')
Inputs may be any that keep to these rules, and one draw needn't show every extreme that they name: Each block's 4 lengths sum to at least 384 and at most 512; slots may be empty; in every draw some block holds a single sequence of 512 rows. `arrange`: each block's 512 entries are a permutation of 0 to 511.
All inputs are finite; a program needn't handle non-finite values.
Results may differ from a plain program's by a relative error of at most 0.012.
Values may be sent and summed in bfloat16 or wider, within the bound.
A program may use at most 128 MiB of HBM per device.

v0:
```python
import jax
import jax.numpy as jnp
from jax import lax
from jax.sharding import PartitionSpec as P

HEADS = 12
HEAD = 64
NORM_EPSILON = 1e-12
MASK_VALUE = -1e30
ROOT_HALF = 0.7071067811865476


def norm_rows(values, norm_gain, norm_shift):
    center = values - jnp.mean(values, axis=-1, keepdims=True)
    spread = jnp.mean(center * center, axis=-1, keepdims=True)
    return center * lax.rsqrt(spread + NORM_EPSILON) * norm_gain + norm_shift


def gelu_exact(values):
    return 0.5 * values * (1.0 + lax.erf(values * ROOT_HALF))


def slot_labels(lengths, arrange):
    total_rows = arrange.shape[0]
    slot_ends = jnp.cumsum(lengths[0])
    position = jnp.arange(total_rows, dtype=jnp.int32)
    slot_index = jnp.sum((position[:, None] >= slot_ends[None, :]).astype(jnp.int32), axis=1)
    return jnp.zeros((total_rows,), jnp.int32).at[arrange].set(slot_index)


def matmul(left_side, right_side, pattern):
    return jnp.einsum(pattern, left_side, right_side, preferred_element_type=jnp.float32)


def column_sums(values):
    return jnp.sum(values.astype(jnp.float32), axis=0)


def gather_matrix(block, n_dp, n_fsdp):
    rows, cols = block.shape
    every = lax.all_gather(block, ("dp", "fsdp"), axis=0, tiled=False)
    every = every.reshape(n_dp, n_fsdp, rows, cols).transpose(0, 2, 1, 3)
    return every.reshape(n_dp * rows, n_fsdp * cols)


def scatter_matrix(grad):
    part = lax.psum_scatter(grad.astype(jnp.bfloat16), "dp", scatter_dimension=0, tiled=True)
    part = lax.psum_scatter(part, "fsdp", scatter_dimension=1, tiled=True)
    return part.astype(jnp.float32)


def local(
    n_dp,
    n_fsdp,
    patches,
    cotangent,
    lengths,
    arrange,
    first_gain,
    first_shift,
    project_weight,
    query_bias,
    value_bias,
    output_weight,
    output_bias,
    second_gain,
    second_shift,
    up_weight,
    up_bias,
    down_weight,
    down_bias,
):
    arrived, cot_rows = (
        lax.all_to_all(patches, "dp", split_axis=0, concat_axis=0, tiled=True),
        lax.all_to_all(cotangent, "dp", split_axis=0, concat_axis=0, tiled=True),
    )
    total_rows, width = patches.shape
    labels = slot_labels(lengths, arrange)
    live_rows = (labels < lengths.shape[1]).astype(jnp.float32)[:, None]
    vector_parts = (
        first_gain,
        first_shift,
        query_bias,
        value_bias,
        output_bias,
        second_gain,
        second_shift,
        up_bias,
        down_bias,
    )
    widths = [v.shape[0] for v in vector_parts]
    packed = lax.all_gather(jnp.concatenate(vector_parts)[None], "dp", axis=0, tiled=True)
    vectors = []
    offset = 0
    for w in widths:
        vectors.append(packed[:, offset : offset + w].reshape(-1).astype(jnp.float32))
        offset += w
    (
        gain_one,
        shift_one,
        query_full,
        value_full,
        outbias_full,
        gain_two,
        shift_two,
        upbias_full,
        downbias_full,
    ) = vectors
    project_full = gather_matrix(project_weight, n_dp, n_fsdp)
    output_full = gather_matrix(output_weight, n_dp, n_fsdp)
    up_full = gather_matrix(up_weight, n_dp, n_fsdp)
    down_full = gather_matrix(down_weight, n_dp, n_fsdp)
    inputs = arrived.astype(jnp.float32)
    normed_one = norm_rows(inputs, gain_one, shift_one)
    normed_low = normed_one.astype(jnp.bfloat16)
    joint = jnp.dot(normed_low, project_full, preferred_element_type=jnp.float32)
    queries = (joint[:, :width] + query_full).astype(jnp.bfloat16).reshape(total_rows, HEADS, HEAD)
    key_rows = joint[:, width : 2 * width].astype(jnp.bfloat16).reshape(total_rows, HEADS, HEAD)
    value_rows = (
        (joint[:, 2 * width :] + value_full).astype(jnp.bfloat16).reshape(total_rows, HEADS, HEAD)
    )
    score_scale = HEAD ** (-0.5)
    visible = labels[:, None] == labels[None, :]

    def block_scores():
        raw_scores = matmul(queries, key_rows, "qhe,khe->hqk") * score_scale
        return jnp.where(visible[None], raw_scores, MASK_VALUE)

    scores = block_scores()
    top_score = jnp.max(scores, axis=-1, keepdims=True)
    weights = jnp.exp(scores - top_score)
    totals = jnp.sum(weights, axis=-1, keepdims=True)
    prob_low = (weights / totals).astype(jnp.bfloat16)
    mixed_rows = matmul(prob_low, value_rows, "hqk,khe->qhe")
    log_totals = top_score + jnp.log(totals)
    attended = mixed_rows.astype(jnp.bfloat16).reshape(total_rows, width)
    attn_out = jnp.dot(attended, output_full, preferred_element_type=jnp.float32) + outbias_full
    hidden = inputs + attn_out
    normed_two = norm_rows(hidden, gain_two, shift_two)
    normed_two_low = normed_two.astype(jnp.bfloat16)
    pre_act = jnp.dot(normed_two_low, up_full, preferred_element_type=jnp.float32) + upbias_full
    activated = gelu_exact(pre_act).astype(jnp.bfloat16)
    branch = jnp.dot(activated, down_full, preferred_element_type=jnp.float32) + downbias_full
    encoded_rows = live_rows * (hidden + branch)
    encoded_back = lax.all_to_all(
        encoded_rows.astype(jnp.bfloat16), "dp", split_axis=0, concat_axis=0, tiled=True
    )
    grad_out = live_rows * cot_rows.astype(jnp.float32)
    grad_branch = grad_out.astype(jnp.bfloat16)
    grad_down = matmul(activated, grad_branch, "tf,td->fd")
    grad_downbias = column_sums(grad_branch)
    grad_activ = matmul(grad_branch, down_full, "td,fd->tf")
    grad_pre = jax.vjp(gelu_exact, pre_act)[1](grad_activ)[0].astype(jnp.bfloat16)
    grad_up = matmul(normed_two_low, grad_pre, "td,tf->df")
    grad_upbias = column_sums(grad_pre)
    grad_normed_two = matmul(grad_pre, up_full, "tf,df->td")
    norm_pull_two = jax.vjp(norm_rows, hidden, gain_two, shift_two)[1]
    grad_hidden_part, grad_gain_two, grad_shift_two = norm_pull_two(grad_normed_two)
    grad_hidden = grad_out + grad_hidden_part
    down_low, up_low = (grad_down.astype(jnp.bfloat16), grad_up.astype(jnp.bfloat16))
    grad_hidden, down_low, up_low = lax.optimization_barrier((grad_hidden, down_low, up_low))
    down_part = scatter_matrix(down_low)
    up_part = scatter_matrix(up_low)
    grad_attn = grad_hidden.astype(jnp.bfloat16)
    grad_output = matmul(attended, grad_attn, "td,te->de")
    grad_outbias = column_sums(grad_attn)
    grad_attended = (
        matmul(grad_attn, output_full, "te,de->td")
        .astype(jnp.bfloat16)
        .reshape(total_rows, HEADS, HEAD)
    )
    output_low = grad_output.astype(jnp.bfloat16)
    grad_attended, output_low = lax.optimization_barrier((grad_attended, output_low))
    output_part = scatter_matrix(output_low)
    scores = block_scores()
    prob_full = jnp.exp(scores - log_totals)
    prob_low = prob_full.astype(jnp.bfloat16)
    value_grad = matmul(prob_low, grad_attended, "hqk,qhe->khe")
    grad_prob = matmul(grad_attended, value_rows, "qhe,khe->hqk")
    inner = jnp.sum(prob_full * grad_prob, axis=-1, keepdims=True)
    grad_scores = (prob_full * (grad_prob - inner)).astype(jnp.bfloat16)
    query_grad = matmul(grad_scores, key_rows, "hqk,khe->qhe") * score_scale
    key_grad = matmul(grad_scores, queries, "hqk,qhe->khe") * score_scale
    grad_queries = query_grad.astype(jnp.bfloat16).reshape(total_rows, width)
    grad_keys = key_grad.reshape(total_rows, width).astype(jnp.bfloat16)
    grad_values = value_grad.reshape(total_rows, width).astype(jnp.bfloat16)
    grad_joint = jnp.concatenate([grad_queries, grad_keys, grad_values], axis=1)
    grad_project = matmul(normed_low, grad_joint, "td,tf->df")
    grad_querybias = column_sums(grad_queries)
    grad_valuebias = column_sums(grad_values)
    project_part = scatter_matrix(grad_project)
    grad_normed_one = matmul(grad_joint, project_full, "tf,df->td")
    norm_pull_one = jax.vjp(norm_rows, inputs, gain_one, shift_one)[1]
    grad_input_part, grad_gain_one, grad_shift_one = norm_pull_one(grad_normed_one)
    grad_inputs = grad_hidden + grad_input_part
    grad_back = lax.all_to_all(
        grad_inputs.astype(jnp.bfloat16), "dp", split_axis=0, concat_axis=0, tiled=True
    )
    vector_grads = (
        grad_gain_one,
        grad_shift_one,
        grad_querybias,
        grad_valuebias,
        grad_outbias,
        grad_gain_two,
        grad_shift_two,
        grad_upbias,
        grad_downbias,
    )
    stacked = jnp.concatenate([g.reshape(n_dp, -1) for g in vector_grads], axis=1)
    stacked = stacked + lax.ppermute(
        stacked, "fsdp", [(i, (i + 1) % n_fsdp) for i in range(n_fsdp)]
    )
    mine = lax.psum_scatter(stacked, "dp", scatter_dimension=0, tiled=True)[0]
    sums = []
    offset = 0
    for w in widths:
        sums.append(mine[offset : offset + w])
        offset += w
    (
        g_gain_one,
        g_shift_one,
        g_querybias,
        g_valuebias,
        g_outbias,
        g_gain_two,
        g_shift_two,
        g_upbias,
        g_downbias,
    ) = sums
    return (
        encoded_back,
        grad_back,
        g_gain_one,
        g_shift_one,
        project_part,
        g_querybias,
        g_valuebias,
        output_part,
        g_outbias,
        g_gain_two,
        g_shift_two,
        up_part,
        g_upbias,
        down_part,
        g_downbias,
    )


def solution(mesh):
    n_dp, n_fsdp = (mesh.shape["dp"], mesh.shape["fsdp"])
    rows = P(("dp", "fsdp"), None)
    matrix = P("dp", "fsdp")
    vector = P("dp")

    def step(*args):
        return local(n_dp, n_fsdp, *args)

    return jax.shard_map(
        step,
        mesh=mesh,
        in_specs=(
            rows,
            rows,
            rows,
            P(("dp", "fsdp")),
            vector,
            vector,
            matrix,
            vector,
            vector,
            matrix,
            vector,
            vector,
            vector,
            matrix,
            vector,
            matrix,
            vector,
        ),
        out_specs=(
            rows,
            rows,
            vector,
            vector,
            matrix,
            vector,
            vector,
            matrix,
            vector,
            vector,
            vector,
            matrix,
            vector,
            matrix,
            vector,
        ),
        check_vma=False,
    )
```

profile of v0, /device:TPU:0, one launch (start us, length us, event | category | flops | bytes accessed | tf_op | source)
XLA Modules:
  0.0 716.6 jit_solution(4727964703437797031)
XLA Ops:
  9.5 7.4 %all-to-all-start = ((bf16[16,32,768]{2,1,0:T(8,128)(2,1)}), bf16[16,32,768]{2,1,0:T(8,128)(2,1)S(1)}, u32[]{:S(2)}, u32[]{:S(2)}) async-start(bf16[16,32,768]{2,1,0:T(8,128)(2,1)} %bitcast.168), calls=%async_computation | async-start | bytes 1572864 | tf_op jit(solution)/shard_map/all_to_all | solution.py:74
  21.6 14.6 %all-to-all-done = bf16[16,32,768]{2,1,0:T(8,128)(2,1)S(1)} async-done(((bf16[16,32,768]{2,1,0:T(8,128)(2,1)}), bf16[16,32,768]{2,1,0:T(8,128)(2,1)S(1)}, u32[]{:S(2)}, u32[]{:S(2)}) %all-to-all-start) | async-done | bytes 786464 | tf_op jit(solution)/shard_map/all_to_all | solution.py:74
  36.1 5.6 all-to-all-start.2
  43.6 68.6 %all-reduce = bf16[9216]{0:T(1024)(128)(2,1)S(1)} all-reduce(bf16[9216]{0:T(1024)(128)(2,1)S(1)} %dynamic-update-slice), channel_id=2, replica_groups=mesh['dp'=16,'fsdp'=2] {'dp'}, use_global_device_ids=true, to_apply=%add | all-reduce | flops 9216 | bytes 36864
  119.8 16.1 %all-gather.10.cloned.1.call-done = bf16[1536,1152]{1,0:T(8,128)(2,1)} async-done(((bf16[48,1152]{1,0:T(8,128)(2,1)}), bf16[1536,1152]{1,0:T(8,128)(2,1)}) %all-gather.10.cloned.1.call-update) | async-done | bytes 3538960 | tf_op jit(solution)/shard_map/all_gather | solution.py:41
  135.9 4.7 copy.68
  151.4 3.0 fusion
  155.9 3.6 fusion.28
  160.8 40.3 %all-gather.14.cloned.1.call-done = bf16[1536,1536]{1,0:T(8,128)(2,1)} async-done(((bf16[48,1536]{1,0:T(8,128)(2,1)}), bf16[1536,1536]{1,0:T(8,128)(2,1)}) %all-gather.14.cloned.1.call-update) | async-done | bytes 4718608 | tf_op jit(solution)/shard_map/all_gather | solution.py:41
  201.2 9.4 %copy.74 = bf16[16,2,48,1536]{3,1,2,0:T(2,128)(2,1)} copy(bf16[16,2,48,1536]{3,2,1,0:T(8,128)(2,1)} %bitcast.143) | data formatting | bytes 9437184 | tf_op jit(solution)/shard_map/reshape | solution.py:42
  210.5 5.7 copy.92
  216.3 49.5 %all-gather.16.cloned.1.call-done = bf16[6144,384]{1,0:T(8,128)(2,1)} async-done(((bf16[192,384]{1,0:T(8,128)(2,1)}), bf16[6144,384]{1,0:T(8,128)(2,1)}) %all-gather.16.cloned.1.call-update) | async-done | bytes 4718608 | tf_op jit(solution)/shard_map/all_gather | solution.py:41
  265.8 9.6 %copy.75 = bf16[16,2,192,384]{3,1,2,0:T(2,128)(2,1)} copy(bf16[16,2,192,384]{3,2,1,0:T(8,128)(2,1)} %bitcast.144) | data formatting | bytes 9437184 | tf_op jit(solution)/shard_map/reshape | solution.py:42
  275.4 3.3 copy.93
  281.9 6.7 convert_reduce_fusion
  288.6 4.0 multiply_reduce_fusion.1
  292.6 4.9 convolution_convert_fusion.1
  301.5 4.5 convolution_convert_fusion.2
  306.0 3.0 convolution_convert_fusion.4
  313.2 9.0 %convert_reduce_fusion.4 = (f32[12,64]{1,0:T(8,128)S(1)}, bf16[12,64,512]{2,1,0:T(8,128)(2,1)}) fusion(bf16[512,12,64]{0,2,1:T(8,128)(2,1)} %bitcast.155, f32[12,512]{1,0:T(8,128)S(1)} %log_add_fusion, f32[12,512,512]{1,2,0:T(8,128)} %copy-done, pred[512,512]{0,1:T(8,128)(4,1)S(1)} %broadcast_compare_fusion), kind=kOutput, calls=%fused_computation.51 | convolution fusion | flops 416414976 | bytes 14445568 | tf_op jit(solution)/shard_map/hqk,qhe->khe/dot_general | solution.py:32
  322.2 9.6 %multiply_reduce_fusion = (f32[12,512]{1,0:T(8,128)S(1)}, f32[12,512,512]{1,2,0:T(8,128)}) fusion(f32[12,512]{1,0:T(8,128)S(1)} %log_add_fusion, f32[12,512,512]{1,2,0:T(8,128)} %copy-done, pred[512,512]{0,1:T(8,128)(4,1)S(1)} %broadcast_compare_fusion, bf16[512,12,64]{0,2,1:T(8,128)(2,1)S(1)} %bitcast.156, bf16[512,12,64]{0,2,1:T(8,128)(2,1)S(1)} %bitcast.154), kind=kOutput, calls=%fused_computation.2 | convolution fusion | flops 418375680 | bytes 27049984 | tf_op jit(solution)/shard_map/qhe,khe->hqk/dot_general | solution.py:32
  331.7 7.1 multiply_convert_fusion
  344.1 5.0 fusion.44
  351.6 3.9 convolution_convert_fusion
  357.8 6.9 multiply_convert_fusion.5
  364.7 3.9 all-to-all-start.1
  368.7 39.1 %reduce-scatter.17.cloned.1.call-done = bf16[48,768]{1,0:T(8,128)(2,1)} async-done(((bf16[768,768]{1,0:T(8,128)(2,1)}), bf16[48,768]{1,0:T(8,128)(2,1)}) %reduce-scatter.17.cloned.1.call-update) | async-done | bytes 73744 | tf_op jit(solution)/shard_map/reduce_scatter | solution.py:47
  409.5 69.1 %reduce-scatter.15.cloned.1.call-done = bf16[48,2304]{1,0:T(8,128)(2,1)} async-done(((bf16[768,2304]{1,0:T(8,128)(2,1)}), bf16[48,2304]{1,0:T(8,128)(2,1)}) %reduce-scatter.15.cloned.1.call-update) | async-done | bytes 221200 | tf_op jit(solution)/shard_map/reduce_scatter | solution.py:47
  480.6 3.6 all-to-all-start.3
  484.3 72.6 %reduce-scatter.23.cloned.1.call-done = bf16[192,768]{1,0:T(8,128)(2,1)} async-done(((bf16[3072,768]{1,0:T(8,128)(2,1)}), bf16[192,768]{1,0:T(8,128)(2,1)}) %reduce-scatter.23.cloned.1.call-update) | async-done | bytes 294928 | tf_op jit(solution)/shard_map/reduce_scatter | solution.py:47
  558.9 76.8 %reduce-scatter.19.cloned.1.call-done = bf16[48,3072]{1,0:T(8,128)(2,1)} async-done(((bf16[768,3072]{1,0:T(8,128)(2,1)}), bf16[48,3072]{1,0:T(8,128)(2,1)}) %reduce-scatter.19.cloned.1.call-update) | async-done | bytes 294928 | tf_op jit(solution)/shard_map/reduce_scatter | solution.py:47
  640.5 57.7 %all-reduce.1 = f32[16,576]{1,0:T(8,128)S(1)} all-reduce(f32[16,576]{1,0:T(8,128)S(1)} %add.163), channel_id=7, replica_groups=mesh['dp'=16,'fsdp'=2] {'dp'}, use_global_device_ids=true, to_apply=%region_23.24.clone | all-reduce | flops 9216 | bytes 73728
  (189 shorter events, 72.0 us)
Async XLA Ops:
  7.2 34.7 %copy-start.20 = (u32[32]{0:T(128)S(1)}, u32[32]{0:T(128)}, u32[]{:S(2)}) copy-start(u32[32]{0:T(128)} %constant.44) | copy-start | bytes 388
  7.2 36.0 %copy-start.29 = (bf16[48]{0:T(256)(128)(2,1)S(1)}, bf16[48]{0:T(256)(128)(2,1)}, u32[]{:S(2)}) copy-start(bf16[48]{0:T(256)(128)(2,1)} %param.33) | copy-start | bytes 292
  7.2 36.0 %copy-start.28 = (bf16[192]{0:T(256)(128)(2,1)S(1)}, bf16[192]{0:T(256)(128)(2,1)}, u32[]{:S(2)}) copy-start(bf16[192]{0:T(256)(128)(2,1)} %param.31) | copy-start | bytes 1156
  7.2 36.0 %copy-start.27 = (bf16[48]{0:T(256)(128)(2,1)S(1)}, bf16[48]{0:T(256)(128)(2,1)}, u32[]{:S(2)}) copy-start(bf16[48]{0:T(256)(128)(2,1)} %param.29) | copy-start | bytes 292
  7.2 36.0 %copy-start.26 = (bf16[48]{0:T(256)(128)(2,1)S(1)}, bf16[48]{0:T(256)(128)(2,1)}, u32[]{:S(2)}) copy-start(bf16[48]{0:T(256)(128)(2,1)} %param.28) | copy-start | bytes 292
  7.2 36.0 %copy-start.25 = (bf16[48]{0:T(256)(128)(2,1)S(1)}, bf16[48]{0:T(256)(128)(2,1)}, u32[]{:S(2)}) copy-start(bf16[48]{0:T(256)(128)(2,1)} %param.27) | copy-start | bytes 292
  7.2 36.0 %copy-start.24 = (bf16[48]{0:T(256)(128)(2,1)S(1)}, bf16[48]{0:T(256)(128)(2,1)}, u32[]{:S(2)}) copy-start(bf16[48]{0:T(256)(128)(2,1)} %param.25) | copy-start | bytes 292
  7.3 36.0 %copy-start.23 = (bf16[48]{0:T(256)(128)(2,1)S(1)}, bf16[48]{0:T(256)(128)(2,1)}, u32[]{:S(2)}) copy-start(bf16[48]{0:T(256)(128)(2,1)} %param.24) | copy-start | bytes 292
  7.3 36.0 %copy-start.22 = (bf16[48]{0:T(256)(128)(2,1)S(1)}, bf16[48]{0:T(256)(128)(2,1)}, u32[]{:S(2)}) copy-start(bf16[48]{0:T(256)(128)(2,1)} %param.22) | copy-start | bytes 292
  7.3 36.0 %copy-start.21 = (bf16[48]{0:T(256)(128)(2,1)S(1)}, bf16[48]{0:T(256)(128)(2,1)}, u32[]{:S(2)}) copy-start(bf16[48]{0:T(256)(128)(2,1)} %param.21) | copy-start | bytes 292
  7.3 109.1 %all-gather.12.cloned.1.call-start = ((), (), s32[]{:S(2)}) async-start(), calls=%async_computation.18 | async-start | bytes 1216512 | tf_op jit(solution)/shard_map/all_gather | solution.py:41
  8.0 127.9 %all-gather.10.cloned.1.call-start = ((), (), s32[]{:S(2)}) async-start(), calls=%async_computation.17 | async-start | bytes 3649536 | tf_op jit(solution)/shard_map/all_gather | solution.py:41
  8.8 192.4 %all-gather.14.cloned.1.call-start = ((), (), s32[]{:S(2)}) async-start(), calls=%async_computation.19 | async-start | bytes 4866048 | tf_op jit(solution)/shard_map/all_gather | solution.py:41
  9.5 26.6 %all-to-all-start = ((bf16[16,32,768]{2,1,0:T(8,128)(2,1)}), bf16[16,32,768]{2,1,0:T(8,128)(2,1)S(1)}, u32[]{:S(2)}, u32[]{:S(2)}) async-start(bf16[16,32,768]{2,1,0:T(8,128)(2,1)} %bitcast.168), calls=%async_computation | async-start | bytes 1572864 | tf_op jit(solution)/shard_map/all_to_all | solution.py:74
  16.9 248.9 %all-gather.16.cloned.1.call-start = ((), (), s32[]{:S(2)}) async-start(), calls=%async_computation.20 | async-start | bytes 4866048 | tf_op jit(solution)/shard_map/all_gather | solution.py:41
  36.1 77.8 %all-to-all-start.2 = ((bf16[16,32,768]{2,1,0:T(8,128)(2,1)}), bf16[16,32,768]{2,1,0:T(8,128)(2,1)S(1)}, u32[]{:S(2)}, u32[]{:S(2)}) async-start(bf16[16,32,768]{2,1,0:T(8,128)(2,1)} %bitcast.169), calls=%async_computation.2 | async-start | bytes 1572864 | tf_op jit(solution)/shard_map/all_to_all | solution.py:75
  41.8 366.0 %reduce-scatter.17.cloned.1.call-start = ((), (), s32[]{:S(2)}) async-start(), calls=%async_computation.13 | async-start | bytes 1253376 | tf_op jit(solution)/shard_map/reduce_scatter | solution.py:47
  160.5 137.0 %copy-start.5 = (f32[512,768]{1,0:T(8,128)}, f32[512,768]{1,0:T(8,128)S(1)}, u32[]{:S(2)}) copy-start(f32[512,768]{1,0:T(8,128)S(1)} %get-tuple-element.71) | copy-start | bytes 4718596
  313.2 9.0 %copy-start.12 = (bf16[512,768]{0,1:T(8,128)(2,1)S(1)}, bf16[512,768]{0,1:T(8,128)(2,1)}, u32[]{:S(2)}) copy-start(bf16[512,768]{0,1:T(8,128)(2,1)} %copy.76) | copy-start | bytes 2359300
  313.2 18.5 %slice-start = ((s8[12582912]{0:T(1024)(128)(4,1)}), s8[4194304]{0:T(1024)(128)(4,1)S(1)}, s32[]{:S(2)}) async-start(s8[12582912]{0:T(1024)(128)(4,1)} %bitcast.134), calls=%async_computation.24 | async-start | bytes 8388608
  313.2 18.5 %slice-start.1 = ((s8[12582912]{0:T(1024)(128)(4,1)}), s8[4194304]{0:T(1024)(128)(4,1)S(1)}, s32[]{:S(2)}) async-start(s8[12582912]{0:T(1024)(128)(4,1)} %bitcast.134), calls=%async_computation.25 | async-start | bytes 8388608
  322.2 9.6 %slice-start.2 = ((s8[12582912]{0:T(1024)(128)(4,1)}), s8[4194304]{0:T(1024)(128)(4,1)S(1)}, s32[]{:S(2)}) async-start(s8[12582912]{0:T(1024)(128)(4,1)} %bitcast.134), calls=%async_computation.26 | async-start | bytes 8388608
  343.8 134.8 %reduce-scatter.15.cloned.1.call-start = ((), (), s32[]{:S(2)}) async-start(), calls=%async_computation.12 | async-start | bytes 3760128 | tf_op jit(solution)/shard_map/reduce_scatter | solution.py:47
  355.6 201.4 %reduce-scatter.23.cloned.1.call-start = ((), (), s32[]{:S(2)}) async-start(), calls=%async_computation.16 | async-start | bytes 5013504 | tf_op jit(solution)/shard_map/reduce_scatter | solution.py:47
  356.4 279.3 %reduce-scatter.19.cloned.1.call-start = ((), (), s32[]{:S(2)}) async-start(), calls=%async_computation.14 | async-start | bytes 5013504 | tf_op jit(solution)/shard_map/reduce_scatter | solution.py:47
  364.7 116.0 %all-to-all-start.1 = ((bf16[16,32,768]{2,1,0:T(8,128)(2,1)}), bf16[16,32,768]{2,1,0:T(8,128)(2,1)S(1)}, u32[]{:S(2)}, u32[]{:S(2)}) async-start(bf16[16,32,768]{2,1,0:T(8,128)(2,1)} %bitcast.19), calls=%async_computation.1 | async-start | bytes 1572864 | tf_op jit(solution)/shard_map/all_to_all | solution.py:145
  368.6 332.2 %reduce-scatter.27.cloned.1.call-start = ((), (), s32[]{:S(2)}) async-start(), calls=%async_computation.22 | async-start | bytes 294912
  409.5 292.9 %reduce-scatter.25.cloned.1.call-start = ((), (), s32[]{:S(2)}) async-start(), calls=%async_computation.21 | async-start | bytes 884736
  480.6 220.1 %all-to-all-start.3 = ((bf16[16,32,768]{2,1,0:T(8,128)(2,1)}), bf16[16,32,768]{2,1,0:T(8,128)(2,1)S(1)}, u32[]{:S(2)}, u32[]{:S(2)}) async-start(bf16[16,32,768]{2,1,0:T(8,128)(2,1)} %bitcast.32), calls=%async_computation.3 | async-start | bytes 1572864 | tf_op jit(solution)/shard_map/all_to_all | solution.py:196
  484.3 220.0 %reduce-scatter.29.cloned.1.call-start = ((), (), s32[]{:S(2)}) async-start(), calls=%async_computation.23 | async-start | bytes 589824
  558.9 147.2 %reduce-scatter.21.cloned.1.call-start = ((), (), s32[]{:S(2)}) async-start(), calls=%async_computation.15 | async-start | bytes 442368 | tf_op jit(solution)/shard_map/reduce_scatter | solution.py:48
  636.5 4.1 collective-permute-start
  (20 other events, 66.9 us)
Sparse Core Ops, SparseCore 0:
  11.0 62.0 all-gather.11
  76.0 59.8 all-gather.9
  138.8 62.2 all-gather.13
  203.9 61.8 all-gather.15
  343.9 63.8 reduce-scatter.16
  411.5 67.0 reduce-scatter.14
  482.5 74.4 reduce-scatter.22
  560.8 74.8 reduce-scatter.18
  638.5 10.1 reduce-scatter.26
  651.4 15.3 reduce-scatter.24
  669.6 13.1 reduce-scatter.28
  684.9 12.0 reduce-scatter.20
where the time goes:
time: 720 us; the launch traced here: 717 us
  waiting for transfers between devices  385 us (53%)
  blocking collectives  126 us (18%)
  matrix products  75.5 us (10%)
  local copies, waits for them, and re-layouts  66.3 us (9%)
  other arithmetic  25.1 us (3%)
  starting transfers between devices  22.8 us (3%)
  between operations  15.8 us (2%)
    reduce_scatter x4, waiting for transfers between devices, scatter_matrix(): lax.psum_scatter(grad.astype(jnp.bfloat16), 'dp', scatter_dimension=0, ti...  258 us
    unnamed x2, blocking collectives  126 us
    all_gather x4, waiting for transfers between devices, gather_matrix(): every = lax.all_gather(block, ('dp', 'fsdp'), axis=0, tiled=False)  106 us
    dot_general x14, matrix products, matmul(): jnp.einsum(pattern, left_side, right_side, preferred_element_type=jnp.flo...  63 us
    unnamed x85, local copies, waits for them, and re-layouts  27 us
    reshape x4, local copies, waits for them, and re-layouts, gather_matrix(): every = every.reshape(n_dp, n_fsdp, rows, cols).transpose(0, 2, 1, 3)  25.9 us
    all_to_all x1, waiting for transfers between devices, local(): lax.all_to_all(patches, 'dp', split_axis=0, concat_axis=0, tiled=True)  14.6 us
  transfers between devices with their start and end apart: 17, of which 9 were waited for; matrix products, arithmetic and copies ran while one was open for 12% of the time, Pallas kernels for 0%

commit v1 on v0

--- a/solution.py
+++ b/solution.py
@@ -8,6 +8,18 @@
 NORM_EPSILON = 1e-12
 MASK_VALUE = -1e30
 ROOT_HALF = 0.7071067811865476
+
+
+def rotated_exchange(array, axis, split, join):
+    ways, here = (lax.axis_size(axis), lax.axis_index(axis))
+    width = array.shape[split] // ways
+    turned = jnp.roll(array, -here * width, axis=split)
+    got = [lax.slice_in_dim(turned, 0, width, axis=split)]
+    for far in range(1, ways):
+        sent = lax.slice_in_dim(turned, far * width, (far + 1) * width, axis=split)
+        got.append(lax.ppermute(sent, axis, [(d, (d + far) % ways) for d in range(ways)]))
+    line = jnp.concatenate(got[::-1], axis=join)
+    return jnp.roll(line, (here + 1) * got[0].shape[join], axis=join)
 
 
 def norm_rows(values, norm_gain, norm_shift):
@@ -71,7 +83,7 @@
     down_bias,
 ):
     arrived, cot_rows = (
-        lax.all_to_all(patches, "dp", split_axis=0, concat_axis=0, tiled=True),
+        rotated_exchange(patches, "dp", 0, 0),
         lax.all_to_all(cotangent, "dp", split_axis=0, concat_axis=0, tiled=True),
     )
     total_rows, width = patches.shape

time: 720 us -> 686 us (0.953)
  waiting for transfers between devices: 385 us -> 315 us
  starting transfers between devices: 22.8 us -> 51.7 us
  local copies, waits for them, and re-layouts: 66.3 us -> 74.6 us
    all_gather x4, waiting for transfers between devices: 106 us -> 63.4 us  [gather_matrix(): every = lax.all_gather(block, ('dp', 'fsdp'), axis=0, tiled=False)]
    reduce_scatter x4, waiting for transfers between devices: 258 us -> 220 us  [scatter_matrix(): lax.psum_scatter(grad.astype(jnp.bfloat16), 'dp', scatter_dimension=0, ti...]
    ppermute x0 -> x15, starting transfers between devices: none -> 34.4 us  [rotated_exchange(): lax.ppermute(sent, axis, [(d, (d + far) % ways) for d in range(ways)])]
    ppermute x0 -> x15, waiting for transfers between devices: none -> 25.1 us  [rotated_exchange(): lax.ppermute(sent, axis, [(d, (d + far) % ways) for d in range(ways)])]
    all_to_all x1 -> x0, waiting for transfers between devices: 14.6 us -> none  [local(): lax.all_to_all(patches, 'dp', split_axis=0, concat_axis=0, tiled=True)]
    all_to_all x1 -> x0, starting transfers between devices: 7.43 us -> none  [local(): lax.all_to_all(patches, 'dp', split_axis=0, concat_axis=0, tiled=True)]
    unnamed x85 -> x128, local copies, waits for them, and re-layouts: 27 us -> 30 us
  transfers between devices with their start and end apart: 17 -> 31, of which waited for: 9 -> 17; matrix products, arithmetic and copies ran while one was open for 12% -> 18% of each run, Pallas kernels for 0% -> 0%
where the time goes in v1:
time: 686 us; the launch traced here: 680 us
  waiting for transfers between devices  315 us (46%)
  blocking collectives  121 us (18%)
  local copies, waits for them, and re-layouts  74.6 us (11%)
  matrix products  72.7 us (11%)
  starting transfers between devices  51.7 us (8%)
  other arithmetic  29.4 us (4%)
  between operations  16.2 us (2%)
    reduce_scatter x4, waiting for transfers between devices, scatter_matrix(): lax.psum_scatter(grad.astype(jnp.bfloat16), 'dp', scatter_dimension=0, ti...  220 us
    unnamed x2, blocking collectives  121 us
    all_gather x4, waiting for transfers between devices, gather_matrix(): every = lax.all_gather(block, ('dp', 'fsdp'), axis=0, tiled=False)  63.4 us
    dot_general x14, matrix products, matmul(): jnp.einsum(pattern, left_side, right_side, preferred_element_type=jnp.flo...  59.6 us
    ppermute x15, starting transfers between devices, rotated_exchange(): lax.ppermute(sent, axis, [(d, (d + far) % ways) for d in range(ways)])  34.4 us
    unnamed x128, local copies, waits for them, and re-layouts  30 us
    reshape x4, local copies, waits for them, and re-layouts, gather_matrix(): every = every.reshape(n_dp, n_fsdp, rows, cols).transpose(0, 2, 1, 3)  25.9 us
    ppermute x15, waiting for transfers between devices, rotated_exchange(): lax.ppermute(sent, axis, [(d, (d + far) % ways) for d in range(ways)])  25.1 us
  transfers between devices with their start and end apart: 31, of which 17 were waited for; matrix products, arithmetic and copies ran while one was open for 18% of the time, Pallas kernels for 0%

profile of v1, /device:TPU:0, one launch (start us, length us, event | category | flops | bytes accessed | tf_op | source)
XLA Modules:
  0.0 680.3 jit_solution(10080293573523621707)
XLA Ops:
  9.5 7.6 %all-to-all-start.1 = ((bf16[16,32,768]{2,1,0:T(8,128)(2,1)}), bf16[16,32,768]{2,1,0:T(8,128)(2,1)S(1)}, u32[]{:S(2)}, u32[]{:S(2)}) async-start(bf16[16,32,768]{2,1,0:T(8,128)(2,1)} %bitcast.137), calls=%async_computation.1 | async-start | bytes 1572864 | tf_op jit(solution)/shard_map/all_to_all | solution.py:87
  28.0 63.1 %all-reduce = bf16[9216]{0:T(1024)(128)(2,1)S(1)} all-reduce(bf16[9216]{0:T(1024)(128)(2,1)S(1)} %dynamic-update-slice), channel_id=2, replica_groups=mesh['dp'=16,'fsdp'=2] {'dp'}, use_global_device_ids=true, to_apply=%add | all-reduce | flops 9216 | bytes 36864
  105.5 3.5 collective-permute-done.2
  109.0 4.3 collective-permute-done.3
  117.0 4.6 collective-permute-start.5
  123.4 6.8 %collective-permute-start.6 = (bf16[32,768]{1,0:T(8,128)(2,1)S(1)}, bf16[32,768]{1,0:T(8,128)(2,1)S(1)}, u32[]{:S(2)}, u32[]{:S(2)}) collective-permute-start(bf16[32,768]{1,0:T(8,128)(2,1)S(1)} %get-tuple-element.56), channel_id=1, source_target_pairs={{0,18},{2,20},{4,22},{6,24},{8,26},{10,28},{12,30},{14,0},{16,2},{... | collective-permute-start | bytes 147464 | tf_op jit(solution)/shard_map/ppermute | solution.py:20
  141.7 4.7 collective-permute-start.9
  148.2 4.1 collective-permute-start.10
  160.5 4.8 copy.68
  180.6 3.6 fusion.24
  185.5 13.8 %all-gather.14.cloned.1.call-done = bf16[1536,1536]{1,0:T(8,128)(2,1)} async-done(((bf16[48,1536]{1,0:T(8,128)(2,1)}), bf16[1536,1536]{1,0:T(8,128)(2,1)}) %all-gather.14.cloned.1.call-update) | async-done | bytes 4718608 | tf_op jit(solution)/shard_map/all_gather | solution.py:53
  199.3 9.4 %copy.74 = bf16[16,2,48,1536]{3,1,2,0:T(2,128)(2,1)} copy(bf16[16,2,48,1536]{3,2,1,0:T(8,128)(2,1)} %bitcast.112) | data formatting | bytes 9437184 | tf_op jit(solution)/shard_map/reshape | solution.py:54
  208.7 5.7 copy.92
  214.5 49.5 %all-gather.16.cloned.1.call-done = bf16[6144,384]{1,0:T(8,128)(2,1)} async-done(((bf16[192,384]{1,0:T(8,128)(2,1)}), bf16[6144,384]{1,0:T(8,128)(2,1)}) %all-gather.16.cloned.1.call-update) | async-done | bytes 4718608 | tf_op jit(solution)/shard_map/all_gather | solution.py:53
  264.0 9.5 %copy.75 = bf16[16,2,192,384]{3,1,2,0:T(2,128)(2,1)} copy(bf16[16,2,192,384]{3,2,1,0:T(8,128)(2,1)} %bitcast.113) | data formatting | bytes 9437184 | tf_op jit(solution)/shard_map/reshape | solution.py:54
  273.5 3.3 copy.93
  280.1 6.6 convert_reduce_fusion
  286.7 4.0 multiply_reduce_fusion.1
  290.7 4.9 convolution_convert_fusion.1
  299.7 4.5 convolution_convert_fusion.2
  311.4 13.5 %multiply_reduce_fusion = (f32[12,512]{1,0:T(8,128)S(1)}, f32[12,512,512]{1,2,0:T(8,128)}) fusion(f32[12,512]{1,0:T(8,128)S(1)} %log_add_fusion, f32[12,512,512]{1,2,0:T(8,128)} %copy-done, pred[512,512]{0,1:T(8,128)(4,1)S(1)} %broadcast_compare_fusion, bf16[512,12,64]{0,2,1:T(8,128)(2,1)} %bitcast.124, bf16[512,12,64]{0,2,1:T(8,128)(2,1)} %bitcast.123), kind=kOutput, calls=%fused_computation.2 | convolution fusion | flops 418375680 | bytes 27049984 | tf_op jit(solution)/shard_map/qhe,khe->hqk/dot_general | solution.py:44
  324.9 10.8 %multiply_convert_fusion = bf16[12,512,512]{1,2,0:T(8,128)(2,1)S(1)} fusion(f32[12,512,512]{1,2,0:T(8,128)} %get-tuple-element.87, f32[12,512]{1,0:T(8,128)S(1)} %get-tuple-element.86, f32[12,512]{1,0:T(8,128)S(1)} %log_add_fusion, f32[12,512,512]{1,2,0:T(8,128)} %copy-done, pred[512,512]{0,1:T(8,128)(4,1)S(1)} %broadcast_compare_fusion), kind=kLoop, calls=%fused_computation.1 | loop fusion | flops 18874368 | bytes 31768576 | tf_op jit(solution)/shard_map/convert_element_type | solution.py:193
  342.5 4.1 convolution_convert_fusion
  348.2 7.3 %multiply_convert_fusion.5 = bf16[512,768]{1,0:T(8,128)(2,1)} fusion(f32[512,768]{1,0:T(8,128)} %copy-done.5, bf16[512,3072]{1,0:T(8,128)(2,1)} %get-tuple-element.41, bf16[3072,768]{1,0:T(8,128)(2,1)} %bitcast.115, f32[768]{0:T(1024)S(1)} %reshape.365, f32[512]{0:T(512)S(1)} %copy-done.24), kind=kOutput, calls=%fused_computation.58 | convolution fusion | flops 2417491968 | bytes 10228736 | tf_op jit(solution)/shard_map/dot_general | solution.py:155
  355.5 3.9 all-to-all-start
  359.7 5.1 fusion.45
  366.8 4.3 reduce-scatter.17.cloned.1.call-done
  372.8 69.3 %reduce-scatter.15.cloned.1.call-done = bf16[48,2304]{1,0:T(8,128)(2,1)} async-done(((bf16[768,2304]{1,0:T(8,128)(2,1)}), bf16[48,2304]{1,0:T(8,128)(2,1)}) %reduce-scatter.15.cloned.1.call-update) | async-done | bytes 221200 | tf_op jit(solution)/shard_map/reduce_scatter | solution.py:59
  447.0 3.6 all-to-all-start.2
  450.7 69.9 %reduce-scatter.23.cloned.1.call-done = bf16[192,768]{1,0:T(8,128)(2,1)} async-done(((bf16[3072,768]{1,0:T(8,128)(2,1)}), bf16[192,768]{1,0:T(8,128)(2,1)}) %reduce-scatter.23.cloned.1.call-update) | async-done | bytes 294928 | tf_op jit(solution)/shard_map/reduce_scatter | solution.py:59
  522.5 76.8 %reduce-scatter.19.cloned.1.call-done = bf16[48,3072]{1,0:T(8,128)(2,1)} async-done(((bf16[768,3072]{1,0:T(8,128)(2,1)}), bf16[48,3072]{1,0:T(8,128)(2,1)}) %reduce-scatter.19.cloned.1.call-update) | async-done | bytes 294928 | tf_op jit(solution)/shard_map/reduce_scatter | solution.py:59
  604.1 57.7 %all-reduce.1 = f32[16,576]{1,0:T(8,128)S(1)} all-reduce(f32[16,576]{1,0:T(8,128)S(1)} %add.165), channel_id=7, replica_groups=mesh['dp'=16,'fsdp'=2] {'dp'}, use_global_device_ids=true, to_apply=%region_23.25.clone | all-reduce | flops 9216 | bytes 73728
  (260 shorter events, 119.6 us)
Async XLA Ops:
  7.2 149.9 %all-gather.12.cloned.1.call-start = ((), (), s32[]{:S(2)}) async-start(), calls=%async_computation.17 | async-start | bytes 1216512 | tf_op jit(solution)/shard_map/all_gather | solution.py:53
  7.9 152.6 %all-gather.10.cloned.1.call-start = ((), (), s32[]{:S(2)}) async-start(), calls=%async_computation.16 | async-start | bytes 3649536 | tf_op jit(solution)/shard_map/all_gather | solution.py:53
  8.7 190.7 %all-gather.14.cloned.1.call-start = ((), (), s32[]{:S(2)}) async-start(), calls=%async_computation.18 | async-start | bytes 4866048 | tf_op jit(solution)/shard_map/all_gather | solution.py:53
  9.5 146.3 %all-to-all-start.1 = ((bf16[16,32,768]{2,1,0:T(8,128)(2,1)}), bf16[16,32,768]{2,1,0:T(8,128)(2,1)S(1)}, u32[]{:S(2)}, u32[]{:S(2)}) async-start(bf16[16,32,768]{2,1,0:T(8,128)(2,1)} %bitcast.137), calls=%async_computation.1 | async-start | bytes 1572864 | tf_op jit(solution)/shard_map/all_to_all | solution.py:87
  17.1 246.9 %all-gather.16.cloned.1.call-start = ((), (), s32[]{:S(2)}) async-start(), calls=%async_computation.19 | async-start | bytes 4866048 | tf_op jit(solution)/shard_map/all_gather | solution.py:53
  18.3 136.6 %collective-permute-start.14 = (bf16[32,768]{1,0:T(8,128)(2,1)S(1)}, bf16[32,768]{1,0:T(8,128)(2,1)S(1)}, u32[]{:S(2)}, u32[]{:S(2)}) collective-permute-start(bf16[32,768]{1,0:T(8,128)(2,1)S(1)} %get-tuple-element.48), channel_id=1, source_target_pairs={{0,2},{2,4},{4,6},{6,8},{8,10},{10,12},{12,14},{14,16},{16,18},{18... | collective-permute-start | bytes 147464 | tf_op jit(solution)/shard_map/ppermute | solution.py:20
  18.7 136.1 %collective-permute-start.13 = (bf16[32,768]{1,0:T(8,128)(2,1)S(1)}, bf16[32,768]{1,0:T(8,128)(2,1)S(1)}, u32[]{:S(2)}, u32[]{:S(2)}) collective-permute-start(bf16[32,768]{1,0:T(8,128)(2,1)S(1)} %get-tuple-element.49), channel_id=1, source_target_pairs={{0,4},{2,6},{4,8},{6,10},{8,12},{10,14},{12,16},{14,18},{16,20},{1... | collective-permute-start | bytes 147464 | tf_op jit(solution)/shard_map/ppermute | solution.py:20
  20.4 134.5 %collective-permute-start.12 = (bf16[32,768]{1,0:T(8,128)(2,1)S(1)}, bf16[32,768]{1,0:T(8,128)(2,1)S(1)}, u32[]{:S(2)}, u32[]{:S(2)}) collective-permute-start(bf16[32,768]{1,0:T(8,128)(2,1)S(1)} %get-tuple-element.50), channel_id=1, source_target_pairs={{0,6},{2,8},{4,10},{6,12},{8,14},{10,16},{12,18},{14,20},{16,22},{... | collective-permute-start | bytes 147464 | tf_op jit(solution)/shard_map/ppermute | solution.py:20
  22.6 131.4 %collective-permute-start.11 = (bf16[32,768]{1,0:T(8,128)(2,1)S(1)}, bf16[32,768]{1,0:T(8,128)(2,1)}, u32[]{:S(2)}, u32[]{:S(2)}) collective-permute-start(bf16[32,768]{1,0:T(8,128)(2,1)S(1)} %get-tuple-element.51), channel_id=1, source_target_pairs={{0,8},{2,10},{4,12},{6,14},{8,16},{10,18},{12,20},{14,22},{16,24},... | collective-permute-start | bytes 147464 | tf_op jit(solution)/shard_map/ppermute | solution.py:20
  24.1 76.7 %collective-permute-start = (bf16[32,768]{1,0:T(8,128)(2,1)S(1)}, bf16[32,768]{1,0:T(8,128)(2,1)S(1)}, u32[]{:S(2)}, u32[]{:S(2)}) collective-permute-start(bf16[32,768]{1,0:T(8,128)(2,1)S(1)} %get-tuple-element.62), channel_id=1, source_target_pairs={{0,30},{2,0},{4,2},{6,4},{8,6},{10,8},{12,10},{14,12},{16,14},{18,... | collective-permute-start | bytes 147464 | tf_op jit(solution)/shard_map/ppermute | solution.py:20
  26.0 345.0 %reduce-scatter.17.cloned.1.call-start = ((), (), s32[]{:S(2)}) async-start(), calls=%async_computation.12 | async-start | bytes 1253376 | tf_op jit(solution)/shard_map/reduce_scatter | solution.py:59
  101.4 4.1 collective-permute-start.1
  105.5 3.5 collective-permute-start.2
  109.0 4.3 collective-permute-start.3
  113.3 3.7 collective-permute-start.4
  117.0 6.4 collective-permute-start.5
  123.4 8.6 %collective-permute-start.6 = (bf16[32,768]{1,0:T(8,128)(2,1)S(1)}, bf16[32,768]{1,0:T(8,128)(2,1)S(1)}, u32[]{:S(2)}, u32[]{:S(2)}) collective-permute-start(bf16[32,768]{1,0:T(8,128)(2,1)S(1)} %get-tuple-element.56), channel_id=1, source_target_pairs={{0,18},{2,20},{4,22},{6,24},{8,26},{10,28},{12,30},{14,0},{16,2},{... | collective-permute-start | bytes 147464 | tf_op jit(solution)/shard_map/ppermute | solution.py:20
  132.0 5.1 collective-permute-start.7
  137.1 4.6 collective-permute-start.8
  141.7 6.5 collective-permute-start.9
  148.2 5.9 collective-permute-start.10
  185.1 110.5 %copy-start.5 = (f32[512,768]{1,0:T(8,128)}, f32[512,768]{1,0:T(8,128)S(1)}, u32[]{:S(2)}) copy-start(f32[512,768]{1,0:T(8,128)S(1)} %get-tuple-element.84) | copy-start | bytes 4718596
  311.3 130.8 %reduce-scatter.15.cloned.1.call-start = ((), (), s32[]{:S(2)}) async-start(), calls=%async_computation.11 | async-start | bytes 3760128 | tf_op jit(solution)/shard_map/reduce_scatter | solution.py:59
  346.6 173.9 %reduce-scatter.23.cloned.1.call-start = ((), (), s32[]{:S(2)}) async-start(), calls=%async_computation.15 | async-start | bytes 5013504 | tf_op jit(solution)/shard_map/reduce_scatter | solution.py:59
  347.4 251.8 %reduce-scatter.19.cloned.1.call-start = ((), (), s32[]{:S(2)}) async-start(), calls=%async_computation.13 | async-start | bytes 5013504 | tf_op jit(solution)/shard_map/reduce_scatter | solution.py:59
  355.5 91.5 %all-to-all-start = ((bf16[16,32,768]{2,1,0:T(8,128)(2,1)}), bf16[16,32,768]{2,1,0:T(8,128)(2,1)S(1)}, u32[]{:S(2)}, u32[]{:S(2)}) async-start(bf16[16,32,768]{2,1,0:T(8,128)(2,1)} %bitcast.139), calls=%async_computation | async-start | bytes 1572864 | tf_op jit(solution)/shard_map/all_to_all | solution.py:157
  359.4 304.9 %reduce-scatter.27.cloned.1.call-start = ((), (), s32[]{:S(2)}) async-start(), calls=%async_computation.21 | async-start | bytes 294912
  372.8 293.2 %reduce-scatter.25.cloned.1.call-start = ((), (), s32[]{:S(2)}) async-start(), calls=%async_computation.20 | async-start | bytes 884736
  447.0 217.3 %all-to-all-start.2 = ((bf16[16,32,768]{2,1,0:T(8,128)(2,1)}), bf16[16,32,768]{2,1,0:T(8,128)(2,1)S(1)}, u32[]{:S(2)}, u32[]{:S(2)}) async-start(bf16[16,32,768]{2,1,0:T(8,128)(2,1)} %bitcast.29), calls=%async_computation.2 | async-start | bytes 1572864 | tf_op jit(solution)/shard_map/all_to_all | solution.py:208
  450.6 217.2 %reduce-scatter.29.cloned.1.call-start = ((), (), s32[]{:S(2)}) async-start(), calls=%async_computation.22 | async-start | bytes 589824
  522.4 147.2 %reduce-scatter.21.cloned.1.call-start = ((), (), s32[]{:S(2)}) async-start(), calls=%async_computation.14 | async-start | bytes 442368 | tf_op jit(solution)/shard_map/reduce_scatter | solution.py:60
  600.0 4.1 collective-permute-start.15
  (48 other events, 410.2 us)
Sparse Core Ops, SparseCore 0:
  10.9 58.9 all-gather.11
  72.9 59.6 all-gather.9
  135.5 63.7 all-gather.13
  202.1 61.8 all-gather.15
  311.5 59.5 reduce-scatter.16
  374.8 67.3 reduce-scatter.14
  446.0 74.5 reduce-scatter.22
  524.4 74.8 reduce-scatter.18
  602.0 10.2 reduce-scatter.26
  614.4 15.3 reduce-scatter.24
  632.6 13.1 reduce-scatter.28
  647.9 12.1 reduce-scatter.20
